TPU v7x, 32 devices: a whole 2x2x4 slice. The times are simulated.
32 devices in a mesh: groups: 2 (over y), tok: 8 (over z, core), head: 2 (over x), pair: 1.
Axes of the slice: x: 2, y: 2, z: 4, core: 2. Of those that a mesh axis runs over, the one named last changes fastest.
Arguments:
- queries: bfloat16 [2048, 4096], P(('groups', 'tok'), ('head', 'pair')), parts along dimension 0, may hold values from -6 to 6
- keys_values: bfloat16 [2048, 1024], P(('groups', 'tok'), ('head', 'pair')), parts along dimension 0, may hold values from -6 to 6
- sink_logits: float32 [64], P(('head', 'pair')), may hold values from -2 to 3
- residual: bfloat16 [2048, 2880], P(('groups', 'tok')), parts along dimension 0, may hold values from -60 to 60
- out_weight: bfloat16 [4096, 2880], P(('head', 'pair')), may hold values from -0.09375 to 0.09375
- norm_gain: float32 [2880], replicated, may hold values from 0.5 to 1.5
- expert_ids: int32 [2048, 4], P(('groups', 'tok')), parts along dimension 0, may hold values from 0 to 7, all different within a row; in each aligned block of 128 rows (0 to 127, 128 to 255, ...) at most 80 rows name the same one
- route_weights: float32 [2048, 4], P(('groups', 'tok')), parts along dimension 0, may hold values from 0.1 to 1
- gate_up: bfloat16 [8, 2880, 2, 1440], P('tok', None, None, ('head', 'pair')), may hold values from -0.109375 to 0.109375
- down_weight: bfloat16 [8, 1440, 2880], P('tok', ('head', 'pair')), may hold values from -0.21875 to 0.21875
Outputs:
- layer_output: bfloat16 [2048, 2880], P(('groups', 'tok'), ('head', 'pair')), parts along dimension 0
There are 2 independent parts, one for each index of `groups`. A program takes and returns all parts, laid end to end along the dimension named above; an argument that names none is the same for every part. Nothing has to cross between parts.
Inputs may be any that keep to these rules, and one draw needn't show every extreme that they name: `expert_ids`: in each aligned block of 128 rows (the rows of one index of tok), a row names 4 different experts and no expert is named by more than 80 rows.
All inputs are finite; a program needn't handle non-finite values.
Results may differ from a plain program's by a relative error of at most 0.01.
Values may be sent and summed in bfloat16 or wider, within the bound.
A program may use at most 128 MiB of HBM per device.

v0:
```python
import jax
import jax.numpy as jnp
from jax import lax
from jax.sharding import PartitionSpec as P

HEAD_DIM = 64


def slot_places(expert_ids, experts, capacity):
    tok_rows = expert_ids.shape[0]
    fanout = expert_ids.shape[1]
    flat_ids = expert_ids.reshape(-1)
    one_hot = (flat_ids[:, None] == jnp.arange(experts, dtype=jnp.int32)[None, :]).astype(jnp.int32)
    earlier = jnp.cumsum(one_hot, axis=0) - one_hot
    ranking = jnp.sum(earlier * one_hot, axis=1)
    targets = flat_ids * capacity + ranking
    sources = jnp.arange(tok_rows * fanout, dtype=jnp.int32) // fanout
    table = jnp.full((experts * capacity,), tok_rows, jnp.int32).at[targets].set(sources)
    return (targets.reshape(tok_rows, fanout), table)


def active_rows(flat_rows, gate_up):
    local_hidden = gate_up.shape[-1]
    both_columns = gate_up.reshape(flat_rows.shape[-1], 2 * local_hidden)
    both = jnp.dot(flat_rows, both_columns, preferred_element_type=jnp.float32)
    gate_part = both[:, :local_hidden]
    up_part = both[:, local_hidden:]
    return (gate_part * jax.nn.sigmoid(1.702 * gate_part) * (up_part + 1.0)).astype(jnp.bfloat16)


def per_device(
    queries,
    keys_values,
    sink_logits,
    residual,
    out_weight,
    norm_gain,
    expert_ids,
    route_weights,
    gate_up,
    down_weight,
):
    tok_rows = queries.shape[0]
    kv_groups = keys_values.shape[1] // (2 * HEAD_DIM)
    local_heads = queries.shape[1] // HEAD_DIM
    repeat = local_heads // kv_groups
    position = lax.axis_index("tok") * tok_rows + jnp.arange(tok_rows, dtype=jnp.int32)
    grouped = queries.reshape(tok_rows, kv_groups, repeat, HEAD_DIM)
    start_max = jnp.broadcast_to(
        sink_logits.reshape(kv_groups, repeat)[:, :, None], (kv_groups, repeat, tok_rows)
    )
    start_totals = jnp.ones((kv_groups, repeat, tok_rows), jnp.float32)
    start_accum = jnp.zeros((kv_groups, repeat, tok_rows, HEAD_DIM), jnp.float32)
    key_piece = lax.all_gather(keys_values, "tok", axis=0, tiled=True)
    totals = start_totals
    accum = start_accum
    count = key_piece.shape[0]
    split_piece = key_piece.reshape(count, kv_groups, 2, HEAD_DIM)
    scores = (
        jnp.einsum(
            "tgrd,ngd->grtn", grouped, split_piece[:, :, 0], preferred_element_type=jnp.float32
        )
        * 0.125
    )
    key_position = jnp.arange(count, dtype=jnp.int32)
    allowed = key_position[None, :] <= position[:, None]
    scores = jnp.where(allowed, scores, jnp.float32(-1e30))
    new_max = jnp.maximum(start_max, jnp.max(scores, axis=-1))
    decay = jnp.exp(start_max - new_max)
    weights = jnp.exp(scores - new_max[..., None])
    totals = totals * decay + jnp.sum(weights, axis=-1)
    update = jnp.einsum(
        "grtn,ngd->grtd",
        weights.astype(jnp.bfloat16),
        split_piece[:, :, 1],
        preferred_element_type=jnp.float32,
    )
    accum = accum * decay[..., None] + update
    final_max, totals, accum = (new_max, totals, accum)
    attended = (accum / totals[..., None]).astype(jnp.bfloat16)
    attended = jnp.transpose(attended, (2, 0, 1, 3)).reshape(tok_rows, local_heads * HEAD_DIM)
    width = out_weight.shape[1]
    experts = lax.axis_size("tok")
    fanout = expert_ids.shape[1]
    capacity = min(tok_rows, tok_rows * fanout * 5 // (4 * experts))
    targets, table = slot_places(expert_ids, experts, capacity)
    share = width // lax.axis_size(("head", "pair"))
    column_start = lax.axis_index(("head", "pair")) * share
    partial_value = jnp.dot(attended, out_weight, preferred_element_type=jnp.float32)
    projected = lax.psum(partial_value.astype(jnp.bfloat16), ("head", "pair")).astype(jnp.float32)
    stream = residual.astype(jnp.float32) + projected
    inverse = lax.rsqrt(jnp.mean(stream * stream, axis=-1, keepdims=True) + 1e-05)
    normed = (stream * inverse * norm_gain).astype(jnp.bfloat16)
    padded = jnp.concatenate([normed, jnp.zeros((1, width), jnp.bfloat16)], axis=0)
    outgoing = padded[table].reshape(experts, capacity, width)
    received = lax.all_to_all(outgoing, "tok", split_axis=0, concat_axis=0, tiled=True)
    shape_in = received.shape
    active = active_rows(received.reshape(-1, shape_in[-1]), gate_up)
    partial_value = jnp.dot(active, down_weight[0], preferred_element_type=jnp.float32)
    partial_out = partial_value.reshape(shape_in[:-1] + (partial_value.shape[-1],))
    stream_share = lax.dynamic_slice_in_dim(stream, column_start, share, 1)
    expert_out = lax.psum_scatter(
        partial_out.astype(jnp.bfloat16), ("head", "pair"), scatter_dimension=2, tiled=True
    )
    returned = lax.all_to_all(expert_out, "tok", split_axis=0, concat_axis=0, tiled=True)
    flat_out = returned.reshape(experts * capacity, share)
    picked = flat_out[targets]
    mixture = jnp.sum(route_weights[:, :, None] * picked.astype(jnp.float32), axis=1)
    return (stream_share + mixture).astype(jnp.bfloat16)


def solution(mesh):
    placed = (
        P(("groups", "tok"), ("head", "pair")),
        P(("groups", "tok"), ("head", "pair")),
        P(("head", "pair")),
        P(("groups", "tok"), None),
        P(("head", "pair"), None),
        P(),
        P(("groups", "tok"), None),
        P(("groups", "tok"), None),
        P("tok", None, None, ("head", "pair")),
        P("tok", ("head", "pair"), None),
    )
    return jax.shard_map(
        per_device,
        mesh=mesh,
        in_specs=placed,
        out_specs=P(("groups", "tok"), ("head", "pair")),
        check_vma=False,
    )
```

profile of v0, /device:TPU:0, one launch (start us, length us, event | category | flops | bytes accessed | tf_op | source)
XLA Modules:
  0.0 360.1 jit_solution(5080762425905200024)
XLA Ops:
  6.5 0.0 all-gather.2.cloned.1.call-start
  6.5 1.7 copy.27
  8.2 0.0 all-gather.2.cloned.1.call-update
  8.2 0.0 all-reduce.3.cloned.1.call-start
  8.3 0.8 copy.33
  9.1 0.1 eq.29
  9.2 0.1 eq.25
  9.3 1.3 copy.29
  10.6 0.7 broadcast_in_dim.20
  11.4 1.1 reduce-window.6
  12.5 0.2 slice_reduce_fusion
  12.8 0.1 fusion.19
  12.8 0.1 reduce_sum.44
  13.0 0.1 iota_compare_fusion
  13.1 22.5 %all-gather.2.cloned.1.call-done = bf16[1024,512]{0,1:T(8,128)(2,1)} async-done(((bf16[128,512]{0,1:T(8,128)(2,1)}), bf16[1024,512]{0,1:T(8,128)(2,1)}) %all-gather.2.cloned.1.call-update) | async-done | bytes 1048592 | tf_op jit(solution)/shard_map/all_gather | solution.py:54
  35.6 8.1 %fusion.2 = (f32[4,8,128]{2,1,0:T(8,128)S(1)}, f32[4,1024,128,8]{2,1,3,0:T(8,128)}) fusion(pred[128,1024]{0,1:T(8,128)(4,1)S(1)} %iota_compare_fusion, bf16[128,4,8,64]{0,3,2,1:T(8,128)(2,1)S(1)} %bitcast.78, bf16[1024,4,2,64]{0,3,2,1:T(8,128)(2,1)} %bitcast.80), kind=kOutput, calls=%fused_computation.7 | convolution fusion | flops 549449728 | bytes 17973248 | tf_op jit(solution)/shard_map/tgrd,ngd->grtn/dot_general | solution.py:60
  43.6 0.1 broadcast_maximum_fusion
  43.7 0.0 copy-start.1
  43.7 9.3 %fusion = f32[4,8,128]{2,1,0:T(8,128)S(1)} fusion(f32[4,1024,128,8]{2,1,3,0:T(8,128)} %get-tuple-element.12, f32[4,8,128]{2,1,0:T(8,128)S(1)} %broadcast_maximum_fusion, pred[128,1024]{0,1:T(8,128)(4,1)S(1)} %iota_compare_fusion), kind=kLoop, calls=%fused_computation.5 | loop fusion | flops 16773120 | bytes 16941056 | tf_op jit(solution)/shard_map/reduce_sum | solution.py:71
  53.0 0.1 multiply_bitcast_fusion
  53.1 0.0 copy-done.1
  53.1 7.8 %divide_convert_fusion = bf16[128,4,8,64]{0,3,2,1:T(8,128)(2,1)S(1)} fusion(f32[4,1024,128,8]{2,1,3,0:T(8,128)} %get-tuple-element.12, f32[4,8,128]{2,1,0:T(8,128)S(1)} %broadcast_maximum_fusion, pred[128,1024]{0,1:T(8,128)(4,1)S(1)} %iota_compare_fusion, bf16[1024,4,2,64]{0,3,2,1:T(8,128)(2,1)S(1)} %bitcast.81, f32[128,4,8]{0,2,1:T(8,128)S(1)} %get-tuple-element.10, ...), kind=kOutput, calls=%fused_computation.22 | convolution fusion | flops 554434560 | bytes 18006016 | tf_op jit(solution)/shard_map/grtn,ngd->grtd/dot_general | solution.py:72
  60.9 0.0 copy-start
  60.9 7.1 %convolution_convert_fusion.1 = bf16[128,2880]{0,1:T(8,128)(2,1)} fusion(bf16[2048,2880]{0,1:T(8,128)(2,1)} %param.14, bf16[128,2048]{0,1:T(8,128)(2,1)S(1)} %bitcast.85), kind=kOutput, calls=%fused_computation.12 | convolution fusion | flops 1510318080 | bytes 13058048 | tf_op jit(solution)/shard_map/dot_general | solution.py:89
  68.0 0.0 copy-start.2
  68.0 0.0 all-reduce.3.cloned.1.call-update
  68.0 0.0 reduce-scatter.4.cloned.1.call-start
  68.1 0.1 mul.93
  68.2 2.6 scatter_custom_fusion
  70.9 29.3 %all-reduce.3.cloned.1.call-done = bf16[128,2880]{0,1:T(8,128)(2,1)} async-done(((bf16[128,2880]{0,1:T(8,128)(2,1)}), bf16[128,2880]{0,1:T(8,128)(2,1)}) %all-reduce.3.cloned.1.call-update) | async-done | bytes 737296 | tf_op jit(solution)/shard_map/psum | solution.py:90
  100.2 0.0 copy-done
  100.2 2.6 convert_add_fusion
  102.8 0.0 copy-done.2
  102.8 1.6 multiply_convert_fusion
  104.4 0.3 copy.46
  104.7 0.1 concatenate.3.clone
  104.8 4.6 %gather_fusion = bf16[640,2880]{1,0:T(8,128)(2,1)} fusion(bf16[129,2880]{1,0:T(8,128)(2,1)S(1)} %concatenate.3.clone, s32[1024]{0:T(1024)S(1)} %pad_clamp_fusion.1), kind=kCustom, calls=%fused_computation | custom fusion | bytes 7375360 | tf_op jit(solution)/shard_map/gather | solution.py:95
  109.4 89.4 %all_to_all.10 = bf16[8,80,2880]{2,1,0:T(8,128)(2,1)S(1)} all-to-all(bf16[8,80,2880]{2,1,0:T(8,128)(2,1)} %bitcast.75), channel_id=1, replica_groups=mesh['groups'=2,'tok'=8,'head'=2,'pair'=1] {'tok'}, dimensions={0} | all-to-all | bytes 7372800 | tf_op jit(solution)/shard_map/all_to_all | solution.py:96
  198.8 9.5 %fusion.28 = f32[640,1440]{0,1:T(8,128)S(1)} fusion(bf16[640,2880]{1,0:T(8,128)(2,1)S(1)} %bitcast.77, bf16[2880,1440]{0,1:T(8,128)(2,1)} %bitcast.84), kind=kOutput, calls=%fused_computation.58 | convolution fusion | flops 5308416000 | bytes 15667200 | tf_op jit(solution)/shard_map/dot_general | solution.py:25
  208.3 0.5 fusion.8
  208.8 1.0 copy.37
  209.9 7.0 %convolution_convert_fusion = bf16[8,80,2880]{2,1,0:T(8,128)(2,1)} fusion(bf16[8,80,720]{2,1,0:T(8,128)(2,1)S(1)} %bitcast.79, bf16[1,720,2880]{2,1,0:T(8,128)(2,1)} %param.19), kind=kOutput, calls=%fused_computation.10 | convolution fusion | flops 2656051200 | bytes 8755200 | tf_op jit(solution)/shard_map/dot_general | solution.py:99
  216.9 8.1 %copy.42 = bf16[8,80,2880]{1,0,2:T(8,128)(2,1)} copy(bf16[8,80,2880]{2,1,0:T(8,128)(2,1)} %convolution_convert_fusion) | data formatting | bytes 7372800
  225.0 9.6 %reshape.137 = bf16[2880,640]{1,0:T(8,128)(2,1)} reshape(bf16[2880,8,80]{2,1,0:T(8,128)(2,1)} %bitcast.74) | data formatting | bytes 7372800
  234.6 0.0 reduce-scatter.4.cloned.1.call-update
  234.6 47.5 %reduce-scatter.4.cloned.1.call-done = bf16[1440,640]{1,0:T(8,128)(2,1)} async-done(((bf16[2880,640]{1,0:T(8,128)(2,1)}), bf16[1440,640]{1,0:T(8,128)(2,1)}) %reduce-scatter.4.cloned.1.call-update) | async-done | bytes 1843216
  282.1 4.8 %reshape.138 = bf16[1440,8,80]{2,1,0:T(8,128)(2,1)S(1)} reshape(bf16[1440,640]{1,0:T(8,128)(2,1)} %reduce-scatter.4.cloned.1.call-done) | data formatting | bytes 3686400
  286.9 0.0 copy-start.3
  286.9 3.5 copy.43
  290.5 4.6 %all-to-all-start.1 = ((bf16[8,80,1440]{2,1,0:T(8,128)(2,1)}), bf16[8,80,1440]{2,1,0:T(8,128)(2,1)S(1)}, u32[]{:S(2)}, u32[]{:S(2)}) async-start(bf16[8,80,1440]{2,1,0:T(8,128)(2,1)} %copy.43), calls=%async_computation.1 | async-start | bytes 3932160 | tf_op jit(solution)/shard_map/all_to_all | solution.py:105
  295.1 0.1 reshape.116
  295.2 0.0 copy-done.3
  295.2 0.1 copy.32
  295.3 46.0 %all-to-all-done.1 = bf16[8,80,1440]{2,1,0:T(8,128)(2,1)S(1)} async-done(((bf16[8,80,1440]{2,1,0:T(8,128)(2,1)}), bf16[8,80,1440]{2,1,0:T(8,128)(2,1)S(1)}, u32[]{:S(2)}, u32[]{:S(2)}) %all-to-all-start.1) | async-done | bytes 1843232 | tf_op jit(solution)/shard_map/all_to_all | solution.py:105
  341.3 3.0 gather_fusion.1
  344.2 2.9 reshape.133
  347.2 3.1 multiply_reduce_fusion
  350.2 1.4 copy.38
  351.6 1.9 add_convert_fusion
  (11 shorter events, 0.1 us)
Async XLA Ops:
  6.5 29.0 %all-gather.2.cloned.1.call-start = ((), (), s32[]{:S(2)}) async-start(), calls=%async_computation.3 | async-start | bytes 1179648 | tf_op jit(solution)/shard_map/all_gather | solution.py:54
  8.2 92.0 %all-reduce.3.cloned.1.call-start = ((), (), s32[]{:S(2)}) async-start(), calls=%async_computation.4 | async-start | bytes 1474560 | tf_op jit(solution)/shard_map/psum | solution.py:90
  43.7 9.3 %copy-start.1 = (bf16[1024,512]{0,1:T(8,128)(2,1)S(1)}, bf16[1024,512]{0,1:T(8,128)(2,1)}, u32[]{:S(2)}) copy-start(bf16[1024,512]{0,1:T(8,128)(2,1)} %all-gather.2.cloned.1.call-done) | copy-start | bytes 3145732
  60.9 39.3 %copy-start = (bf16[128,2880]{0,1:T(8,128)(2,1)S(1)}, bf16[128,2880]{0,1:T(8,128)(2,1)}, u32[]{:S(2)}) copy-start(bf16[128,2880]{0,1:T(8,128)(2,1)} %param.13) | copy-start | bytes 2211844
  68.0 34.8 %copy-start.2 = (f32[2880]{0:T(1024)S(1)}, f32[2880]{0:T(1024)}, u32[]{:S(2)}) copy-start(f32[2880]{0:T(1024)} %param.15) | copy-start | bytes 34564
  68.0 214.1 %reduce-scatter.4.cloned.1.call-start = ((), (), s32[]{:S(2)}) async-start(), calls=%async_computation.5 | async-start | bytes 5529600
  286.9 8.3 %copy-start.3 = (f32[128,4]{0,1:T(4,128)S(1)}, f32[128,4]{0,1:T(4,128)}, u32[]{:S(2)}) copy-start(f32[128,4]{0,1:T(4,128)} %param.17) | copy-start | bytes 6148
  290.5 50.8 %all-to-all-start.1 = ((bf16[8,80,1440]{2,1,0:T(8,128)(2,1)}), bf16[8,80,1440]{2,1,0:T(8,128)(2,1)S(1)}, u32[]{:S(2)}, u32[]{:S(2)}) async-start(bf16[8,80,1440]{2,1,0:T(8,128)(2,1)} %copy.43), calls=%async_computation.1 | async-start | bytes 3932160 | tf_op jit(solution)/shard_map/all_to_all | solution.py:105
Sparse Core Ops, SparseCore 0:
  8.9 26.5 all-gather.1
  68.1 32.0 all-reduce.2
  234.7 47.3 reduce-scatter.3
where the time goes:
time: 361 us; the launch traced here: 360 us
  waiting for transfers between devices  145 us (40%)
  blocking collectives  89.4 us (25%)
  local copies, waits for them, and re-layouts  47.4 us (13%)
  matrix products  39.4 us (11%)
  other arithmetic  20.5 us (6%)
  between operations  13.3 us (4%)
  starting transfers between devices  4.69 us (1%)
    all_to_all x1, blocking collectives, per_device(): lax.all_to_all(outgoing, 'tok', split_axis=0, concat_axis=0, tiled=True)  89.4 us
    unnamed x4, waiting for transfers between devices  47.5 us
    all_to_all x1, waiting for transfers between devices, per_device(): lax.all_to_all(expert_out, 'tok', split_axis=0, concat_axis=0, tiled=True)  46 us
    unnamed x17, local copies, waits for them, and re-layouts  30.3 us
    psum x1, waiting for transfers between devices, per_device(): lax.psum(partial_value.astype(jnp.bfloat16), ('head', 'pair'))  29.3 us
    all_gather x1, waiting for transfers between devices, per_device(): key_piece = lax.all_gather(keys_values, 'tok', axis=0, tiled=True)  22.5 us
    dot_general x1, matrix products, active_rows(): both = jnp.dot(flat_rows, both_columns, preferred_element_type=jnp.float32)  9.46 us
    reduce_sum x1, other arithmetic, per_device(): totals = totals * decay + jnp.sum(weights, axis=-1)  9.26 us
  transfers between devices with their start and end apart: 4, of which 4 were waited for; matrix products, arithmetic and copies ran while one was open for 2% of the time, Pallas kernels for 0%

commit v1 on v0

--- a/solution.py
+++ b/solution.py
@@ -4,6 +4,12 @@
 from jax.sharding import PartitionSpec as P
 
 HEAD_DIM = 64
+
+
+def add_all(x, axis):
+    pieces = lax.all_gather(x, axis, axis=0, tiled=False)
+    total = pieces.sum(axis=0)
+    return total
 
 
 def slot_places(expert_ids, experts, capacity):
@@ -87,7 +93,7 @@
     share = width // lax.axis_size(("head", "pair"))
     column_start = lax.axis_index(("head", "pair")) * share
     partial_value = jnp.dot(attended, out_weight, preferred_element_type=jnp.float32)
-    projected = lax.psum(partial_value.astype(jnp.bfloat16), ("head", "pair")).astype(jnp.float32)
+    projected = add_all(partial_value.astype(jnp.bfloat16), ("head", "pair")).astype(jnp.float32)
     stream = residual.astype(jnp.float32) + projected
     inverse = lax.rsqrt(jnp.mean(stream * stream, axis=-1, keepdims=True) + 1e-05)
     normed = (stream * inverse * norm_gain).astype(jnp.bfloat16)

time: 361 us -> 367 us (1.017)
  other arithmetic: 20.5 us -> 31 us
  waiting for transfers between devices: 145 us -> 138 us
    psum x1 -> x0, waiting for transfers between devices: 29.3 us -> none  [per_device(): lax.psum(partial_value.astype(jnp.bfloat16), ('head', 'pair'))]
    all_gather x0 -> x1, waiting for transfers between devices: none -> 19.8 us  [add_all(): pieces = lax.all_gather(x, axis, axis=0, tiled=False)]
    reduce_sum x0 -> x1, other arithmetic: none -> 15.3 us  [add_all(): total = pieces.sum(axis=0)]
    unnamed x17 -> x21, local copies, waits for them, and re-layouts: 30.3 us -> 29.6 us
where the time goes in v1:
time: 367 us; the launch traced here: 366 us
  waiting for transfers between devices  138 us (38%)
  blocking collectives  89.4 us (24%)
  local copies, waits for them, and re-layouts  49.8 us (14%)
  matrix products  39.5 us (11%)
  other arithmetic  31 us (8%)
  between operations  13.4 us (4%)
  starting transfers between devices  4.68 us (1%)
    all_to_all x1, blocking collectives, per_device(): lax.all_to_all(outgoing, 'tok', split_axis=0, concat_axis=0, tiled=True)  89.4 us
    unnamed x4, waiting for transfers between devices  47.6 us
    all_to_all x1, waiting for transfers between devices, per_device(): lax.all_to_all(expert_out, 'tok', split_axis=0, concat_axis=0, tiled=True)  46 us
    unnamed x21, local copies, waits for them, and re-layouts  29.6 us
    all_gather x1, waiting for transfers between devices, per_device(): key_piece = lax.all_gather(keys_values, 'tok', axis=0, tiled=True)  25.1 us
    all_gather x1, waiting for transfers between devices, add_all(): pieces = lax.all_gather(x, axis, axis=0, tiled=False)  19.8 us
    reduce_sum x1, other arithmetic, add_all(): total = pieces.sum(axis=0)  15.3 us
    dot_general x1, matrix products, active_rows(): both = jnp.dot(flat_rows, both_columns, preferred_element_type=jnp.float32)  9.44 us
  transfers between devices with their start and end apart: 4, of which 4 were waited for; matrix products, arithmetic and copies ran while one was open for 2% of the time, Pallas kernels for 0%

profile of v1, /device:TPU:0, one launch (start us, length us, event | category | flops | bytes accessed | tf_op | source)
XLA Modules:
  0.0 366.2 jit_solution(17279860285508581211)
XLA Ops:
  6.5 0.0 all-gather.4.cloned.1.call-start
  6.5 1.7 copy.30
  8.2 0.0 all-gather.4.cloned.1.call-update
  8.2 0.0 all-gather.6.cloned.1.call-start
  8.3 1.3 copy.32
  9.6 0.7 broadcast_in_dim.20
  10.3 0.1 iota_compare_fusion
  10.4 25.1 %all-gather.4.cloned.1.call-done = bf16[1024,512]{0,1:T(8,128)(2,1)} async-done(((bf16[128,512]{0,1:T(8,128)(2,1)}), bf16[1024,512]{0,1:T(8,128)(2,1)}) %all-gather.4.cloned.1.call-update) | async-done | bytes 1048592 | tf_op jit(solution)/shard_map/all_gather | solution.py:60
  35.6 8.1 %fusion.2 = (f32[4,8,128]{2,1,0:T(8,128)S(1)}, f32[4,1024,128,8]{2,1,3,0:T(8,128)}) fusion(pred[128,1024]{0,1:T(8,128)(4,1)S(1)} %iota_compare_fusion, bf16[128,4,8,64]{0,3,2,1:T(8,128)(2,1)S(1)} %bitcast.80, bf16[1024,4,2,64]{0,3,2,1:T(8,128)(2,1)} %bitcast.82), kind=kOutput, calls=%fused_computation.7 | convolution fusion | flops 549449728 | bytes 17973248 | tf_op jit(solution)/shard_map/tgrd,ngd->grtn/dot_general | solution.py:66
  43.6 0.1 broadcast_maximum_fusion
  43.7 9.4 %fusion = f32[4,8,128]{2,1,0:T(8,128)S(1)} fusion(f32[4,1024,128,8]{2,1,3,0:T(8,128)} %get-tuple-element.12, f32[4,8,128]{2,1,0:T(8,128)S(1)} %broadcast_maximum_fusion, pred[128,1024]{0,1:T(8,128)(4,1)S(1)} %iota_compare_fusion), kind=kLoop, calls=%fused_computation.5 | loop fusion | flops 16773120 | bytes 16941056 | tf_op jit(solution)/shard_map/reduce_sum | solution.py:77
  53.1 0.1 multiply_bitcast_fusion
  53.2 0.0 copy-done.2
  53.2 7.8 %divide_convert_fusion = bf16[128,4,8,64]{0,3,2,1:T(8,128)(2,1)S(1)} fusion(f32[4,1024,128,8]{2,1,3,0:T(8,128)} %get-tuple-element.12, f32[4,8,128]{2,1,0:T(8,128)S(1)} %broadcast_maximum_fusion, pred[128,1024]{0,1:T(8,128)(4,1)S(1)} %iota_compare_fusion, bf16[1024,4,2,64]{0,3,2,1:T(8,128)(2,1)S(1)} %bitcast.83, f32[128,4,8]{0,2,1:T(8,128)S(1)} %get-tuple-element.10, ...), kind=kOutput, calls=%fused_computation.22 | convolution fusion | flops 554434560 | bytes 18006016 | tf_op jit(solution)/shard_map/grtn,ngd->grtd/dot_general | solution.py:78
  61.0 0.0 copy-start.4
  61.0 0.0 copy-start.1
  61.1 7.1 %convolution_convert_fusion.1 = bf16[128,2880]{0,1:T(8,128)(2,1)} fusion(bf16[2048,2880]{0,1:T(8,128)(2,1)} %param.14, bf16[128,2048]{0,1:T(8,128)(2,1)S(1)} %bitcast.87), kind=kOutput, calls=%fused_computation.12 | convolution fusion | flops 1510318080 | bytes 13058048 | tf_op jit(solution)/shard_map/dot_general | solution.py:95
  68.2 0.0 all-gather.6.cloned.1.call-update
  68.2 0.0 reduce-scatter.4.cloned.1.call-start
  68.3 0.0 copy-done.4
  68.3 0.1 copy.37
  68.4 0.1 eq.29
  68.5 0.1 eq.25
  68.6 0.0 copy-done.1
  68.6 0.3 copy.29
  69.0 1.1 reduce-window.6
  70.1 0.2 slice_reduce_fusion
  70.4 0.1 fusion.19
  70.5 0.1 reduce_sum.57
  70.6 0.1 mul.93
  70.7 2.6 scatter_custom_fusion
  73.4 19.8 %all-gather.6.cloned.1.call-done = bf16[256,2880]{0,1:T(8,128)(2,1)} async-done(((bf16[128,2880]{0,1:T(8,128)(2,1)}), bf16[256,2880]{0,1:T(8,128)(2,1)}) %all-gather.6.cloned.1.call-update) | async-done | bytes 1474576 | tf_op jit(solution)/shard_map/all_gather | solution.py:10
  93.2 3.2 reshape.130
  96.4 0.0 copy-start.3
  96.4 15.3 %reduce_sum.53 = bf16[128,2880]{0,1:T(8,128)(2,1)S(1)} reduce(bf16[2,128,2880]{1,0,2:T(2,128)(2,1)S(1)} %reshape.130, bf16[]{:T(256)} %constant.29.clone.1), dimensions={0}, to_apply=%region_2.3 | reduce | flops 368640 | bytes 2211842 | tf_op jit(solution)/shard_map/reduce_sum | solution.py:11
  111.7 0.3 copy.35
  112.0 1.4 convert_add_fusion
  113.4 0.0 copy-done.3
  113.4 0.3 multiply_convert_fusion
  113.7 0.1 concatenate.3
  113.8 4.6 %gather_fusion = bf16[640,2880]{1,0:T(8,128)(2,1)} fusion(bf16[129,2880]{1,0:T(8,128)(2,1)S(1)} %concatenate.3, s32[1024]{0:T(1024)S(1)} %pad_clamp_fusion.1), kind=kCustom, calls=%fused_computation | custom fusion | bytes 7375360 | tf_op jit(solution)/shard_map/gather | solution.py:101
  118.4 89.4 %all_to_all.10 = bf16[8,80,2880]{2,1,0:T(8,128)(2,1)S(1)} all-to-all(bf16[8,80,2880]{2,1,0:T(8,128)(2,1)} %bitcast.77), channel_id=1, replica_groups=mesh['groups'=2,'tok'=8,'head'=2,'pair'=1] {'tok'}, dimensions={0} | all-to-all | bytes 7372800 | tf_op jit(solution)/shard_map/all_to_all | solution.py:102
  207.8 9.4 %fusion.28 = f32[640,1440]{0,1:T(8,128)S(1)} fusion(bf16[640,2880]{1,0:T(8,128)(2,1)S(1)} %bitcast.79, bf16[2880,1440]{0,1:T(8,128)(2,1)} %bitcast.86), kind=kOutput, calls=%fused_computation.58 | convolution fusion | flops 5308416000 | bytes 15667200 | tf_op jit(solution)/shard_map/dot_general | solution.py:31
  217.3 0.5 fusion.8
  217.8 1.0 copy.40
  218.8 7.0 %convolution_convert_fusion = bf16[8,80,2880]{2,1,0:T(8,128)(2,1)} fusion(bf16[8,80,720]{2,1,0:T(8,128)(2,1)S(1)} %bitcast.81, bf16[1,720,2880]{2,1,0:T(8,128)(2,1)} %param.19), kind=kOutput, calls=%fused_computation.10 | convolution fusion | flops 2656051200 | bytes 8755200 | tf_op jit(solution)/shard_map/dot_general | solution.py:105
  225.8 8.1 %copy.45 = bf16[8,80,2880]{1,0,2:T(8,128)(2,1)} copy(bf16[8,80,2880]{2,1,0:T(8,128)(2,1)} %convolution_convert_fusion) | data formatting | bytes 7372800
  234.0 9.6 %reshape.138 = bf16[2880,640]{1,0:T(8,128)(2,1)} reshape(bf16[2880,8,80]{2,1,0:T(8,128)(2,1)} %bitcast.76) | data formatting | bytes 7372800
  243.6 0.0 reduce-scatter.4.cloned.1.call-update
  243.6 47.5 %reduce-scatter.4.cloned.1.call-done = bf16[1440,640]{1,0:T(8,128)(2,1)} async-done(((bf16[2880,640]{1,0:T(8,128)(2,1)}), bf16[1440,640]{1,0:T(8,128)(2,1)}) %reduce-scatter.4.cloned.1.call-update) | async-done | bytes 1843216
  291.1 4.8 %reshape.139 = bf16[1440,8,80]{2,1,0:T(8,128)(2,1)S(1)} reshape(bf16[1440,640]{1,0:T(8,128)(2,1)} %reduce-scatter.4.cloned.1.call-done) | data formatting | bytes 3686400
  295.9 0.0 copy-start.5
  295.9 3.5 copy.46
  299.5 4.6 %all-to-all-start.1 = ((bf16[8,80,1440]{2,1,0:T(8,128)(2,1)}), bf16[8,80,1440]{2,1,0:T(8,128)(2,1)S(1)}, u32[]{:S(2)}, u32[]{:S(2)}) async-start(bf16[8,80,1440]{2,1,0:T(8,128)(2,1)} %copy.46), calls=%async_computation.1 | async-start | bytes 3932160 | tf_op jit(solution)/shard_map/all_to_all | solution.py:111
  304.1 0.1 reshape.116
  304.2 0.0 copy-done.5
  304.2 0.1 copy.36
  304.3 46.0 %all-to-all-done.1 = bf16[8,80,1440]{2,1,0:T(8,128)(2,1)S(1)} async-done(((bf16[8,80,1440]{2,1,0:T(8,128)(2,1)}), bf16[8,80,1440]{2,1,0:T(8,128)(2,1)S(1)}, u32[]{:S(2)}, u32[]{:S(2)}) %all-to-all-start.1) | async-done | bytes 1843232 | tf_op jit(solution)/shard_map/all_to_all | solution.py:111
  350.3 3.0 gather_fusion.1
  353.2 2.9 reshape.134
  356.1 0.0 copy-start
  356.2 2.2 multiply_reduce_fusion
  358.4 0.3 add_convert_fusion
  358.7 0.9 copy.41
  (13 shorter events, 0.1 us)
Async XLA Ops:
  6.5 29.0 %all-gather.4.cloned.1.call-start = ((), (), s32[]{:S(2)}) async-start(), calls=%async_computation.3 | async-start | bytes 1179648 | tf_op jit(solution)/shard_map/all_gather | solution.py:60
  8.2 84.9 %all-gather.6.cloned.1.call-start = ((), (), s32[]{:S(2)}) async-start(), calls=%async_computation.4 | async-start | bytes 2211840 | tf_op jit(solution)/shard_map/all_gather | solution.py:10
  43.7 9.5 %copy-start.2 = (bf16[1024,512]{0,1:T(8,128)(2,1)S(1)}, bf16[1024,512]{0,1:T(8,128)(2,1)}, u32[]{:S(2)}) copy-start(bf16[1024,512]{0,1:T(8,128)(2,1)} %all-gather.4.cloned.1.call-done) | copy-start | bytes 3145732
  61.0 7.2 %copy-start.4 = (s32[128,4]{0,1:T(4,128)S(1)}, s32[128,4]{0,1:T(4,128)}, u32[]{:S(2)}) copy-start(s32[128,4]{0,1:T(4,128)} %param.16) | copy-start | bytes 6148
  61.0 7.5 %copy-start.1 = (bf16[128,2880]{0,1:T(8,128)(2,1)S(1)}, bf16[128,2880]{0,1:T(8,128)(2,1)}, u32[]{:S(2)}) copy-start(bf16[128,2880]{0,1:T(8,128)(2,1)} %param.13) | copy-start | bytes 2211844
  68.2 222.9 %reduce-scatter.4.cloned.1.call-start = ((), (), s32[]{:S(2)}) async-start(), calls=%async_computation.5 | async-start | bytes 5529600
  96.4 17.1 %copy-start.3 = (f32[2880]{0:T(1024)S(1)}, f32[2880]{0:T(1024)}, u32[]{:S(2)}) copy-start(f32[2880]{0:T(1024)} %param.15) | copy-start | bytes 34564
  295.9 8.3 %copy-start.5 = (f32[128,4]{0,1:T(4,128)S(1)}, f32[128,4]{0,1:T(4,128)}, u32[]{:S(2)}) copy-start(f32[128,4]{0,1:T(4,128)} %param.17) | copy-start | bytes 6148
  299.5 50.8 %all-to-all-start.1 = ((bf16[8,80,1440]{2,1,0:T(8,128)(2,1)}), bf16[8,80,1440]{2,1,0:T(8,128)(2,1)S(1)}, u32[]{:S(2)}, u32[]{:S(2)}) async-start(bf16[8,80,1440]{2,1,0:T(8,128)(2,1)} %copy.46), calls=%async_computation.1 | async-start | bytes 3932160 | tf_op jit(solution)/shard_map/all_to_all | solution.py:111
  356.1 2.3 copy-start
Sparse Core Ops, SparseCore 0:
  8.9 26.5 all-gather.3
  68.3 24.8 all-gather.5
  243.7 47.3 reduce-scatter.3
